TPU v7x, 256 devices: a whole 4x4x8 slice. The times are simulated.
256 devices in a mesh: img: 16 (over y, x), row: 16 (over z, core).
Axes of the slice: x: 4, y: 4, z: 8, core: 2. Of those that a mesh axis runs over, the one named last changes fastest.
Arguments:
- latent: bfloat16 [1024, 128, 512], P(('img', 'row')), parts along dimension 0, may hold values from -8 to 8
- attn_gain: float32 [512], replicated, may hold values from 0.5 to 1.5
- attn_shift: float32 [512], replicated, may hold values from -3 to 3
- w_query: bfloat16 [512, 512], replicated, may hold values from -2 to 2
- w_key: bfloat16 [512, 512], replicated, may hold values from -2 to 2
- w_value: bfloat16 [512, 512], replicated, may hold values from -0.25 to 0.25
- w_out: bfloat16 [512, 512], replicated, may hold values from -0.25 to 0.25
- conv_gain: float32 [512], replicated, may hold values from 0.5 to 1.5
- conv_shift: float32 [512], replicated, may hold values from -3 to 3
- w_conv: bfloat16 [3, 3, 512, 512], replicated, may hold values from -0.09375 to 0.09375
- conv_bias: float32 [512], replicated, may hold values from -3 to 3
Outputs:
- encoded: bfloat16 [1024, 128, 512], P(('img', 'row')), parts along dimension 0
There are 16 independent parts, one for each index of `img`. A program takes and returns all parts, laid end to end along the dimension named above; an argument that names none is the same for every part. Nothing has to cross between parts.
All inputs are finite; a program needn't handle non-finite values.
Results may differ from a plain program's by a relative error of at most 0.011.
Values may be sent and summed in bfloat16 or wider, within the bound.
A program may use at most 128 MiB of HBM per device.

v0:
```python
import functools
import math

import jax
import jax.numpy as jnp
from jax import lax
from jax.experimental import pallas as pl
from jax.experimental.pallas import tpu as pltpu
from jax.sharding import PartitionSpec as P

GROUPS = 32
EPS = 1e-06
CHUNK = 128
MESH = pl.DeviceIdType.MESH
LOG2E = math.log2(math.e)
NT = (((1,), (1,)), ((), ()))


def spread_groups(row, ones):
    high = row.astype(jnp.bfloat16).astype(jnp.float32)
    rest = row - high
    mid = rest.astype(jnp.bfloat16).astype(jnp.float32)
    low = rest - mid
    index = lax.broadcasted_iota(jnp.int32, (16, row.shape[1]), 0)
    parts = jnp.where(index == 0, high, jnp.where(index == 1, mid, jnp.where(index == 2, low, 0.0)))
    sums = jnp.dot(parts.astype(jnp.bfloat16), ones, preferred_element_type=jnp.float32)
    return jnp.sum(sums, axis=0, keepdims=True)


def kernel(
    n, wide,
    latent, w_query, w_key, w_value, w_out, w_conv,
    attn_gain, attn_shift, conv_gain, conv_shift, conv_bias,
    out,
    kv, wq, wk, wv, wo, wc, ones, moments, queries, bias, maxima, total, acc, hidden, halo, stacked,
    load_sem, weight_sem, send_sem, recv_sem, stat_send, stat_recv, halo_send, halo_recv,
    result, store_sem,
):
    chunks, chunk, channels = kv.shape[1:]
    rows = chunks * chunk
    deep = n // 2
    lines = rows // wide
    size = channels // GROUPS
    img = lax.axis_index("img")
    r = lax.axis_index("row")
    z = r // 2
    c = r % 2
    partner = r + 1 - 2 * c

    loads = [
        pltpu.make_async_copy(latent.at[k], kv.at[r, k], load_sem.at[k]) for k in range(chunks)
    ]
    for load in loads:
        load.start()
    weights = [
        pltpu.make_async_copy(source, target, weight_sem.at[i])
        for i, (source, target) in enumerate([(w_query, wq), (w_key, wk), (w_value, wv), (w_out, wo)])
    ]
    weights += [
        pltpu.make_async_copy(
            w_conv.at[dy, dx],
            wc.at[dx, pl.ds(dy * channels, channels)],
            weight_sem.at[4 + dy * 3 + dx],
        )
        for dy in range(3)
        for dx in range(3)
    ]
    for weight in weights:
        weight.start()

    barrier = pltpu.get_barrier_semaphore()

    @pl.loop(1, n)
    def _(j):
        pl.semaphore_signal(
            barrier, inc=1, device_id=(img, lax.rem(r + j, n)), device_id_type=MESH
        )

    def piece(way, zb, k):
        b = zb * 2 + c
        target = (r + 2, r - 2, partner)[way]
        return pltpu.make_async_remote_copy(
            src_ref=kv.at[b, k],
            dst_ref=kv.at[b, k],
            send_sem=send_sem.at[way, zb, k],
            recv_sem=recv_sem.at[b, k],
            device_id=(img, target),
            device_id_type=MESH,
        )

    def arrival(b, k):
        return pltpu.make_async_remote_copy(
            src_ref=kv.at[b, k],
            dst_ref=kv.at[b, k],
            send_sem=send_sem.at[0, 0, 0],
            recv_sem=recv_sem.at[b, k],
            device_id=(img, partner),
            device_id_type=MESH,
        )

    def stat_copy(which, j):
        return pltpu.make_async_remote_copy(
            src_ref=moments.at[which, r],
            dst_ref=moments.at[which, r],
            send_sem=stat_send.at[which, j],
            recv_sem=stat_recv.at[which, r],
            device_id=(img, lax.rem(r + j, n)),
            device_id_type=MESH,
        )

    def stat_arrival(which, b):
        return pltpu.make_async_remote_copy(
            src_ref=moments.at[which, b],
            dst_ref=moments.at[which, b],
            send_sem=stat_send.at[which, 0],
            recv_sem=stat_recv.at[which, b],
            device_id=(img, partner),
            device_id_type=MESH,
        )

    def send_own(k):
        @pl.when(z < deep - 1)
        def _():
            piece(0, z, k).start()

        @pl.when(z > 0)
        def _():
            piece(1, z, k).start()

        piece(2, z, k).start()

    def share_moments(which, field):
        mean = jnp.sum(field, axis=0, keepdims=True) * (1.0 / rows)
        offset = field - mean
        square = jnp.sum(offset * offset, axis=0, keepdims=True)
        moments[which, r, 0:1, :] = mean
        moments[which, r, 1:2, :] = square

        @pl.loop(1, n)
        def _(j):
            stat_copy(which, j).start()

    def gather_moments(which):
        @pl.loop(1, n)
        def _(j):
            stat_arrival(which, lax.rem(r + j, n)).wait_recv()

        @pl.loop(1, n)
        def _(j):
            stat_copy(which, j).wait_send()

        every = moments[which]
        means = every[:, 0, :]
        squares = every[:, 1, :]
        centre = spread_groups(jnp.sum(means, axis=0, keepdims=True), ones[...]) * (
            1.0 / (n * size)
        )
        away = means - centre
        whole = jnp.sum(squares + rows * (away * away), axis=0, keepdims=True)
        variance = spread_groups(whole, ones[...]) * (1.0 / (n * size * rows))
        return centre, lax.rsqrt(variance + EPS)

    for load in loads:
        load.wait()
    pl.semaphore_wait(barrier, n - 1)
    send_own(0)
    share_moments(0, kv[r].reshape(rows, channels).astype(jnp.float32))
    for k in range(1, chunks):
        send_own(k)

    left_group = lax.broadcasted_iota(jnp.int32, (channels, channels), 0) // size
    right_group = lax.broadcasted_iota(jnp.int32, (channels, channels), 1) // size
    ones[...] = jnp.where(left_group == right_group, 1.0, 0.0).astype(jnp.bfloat16)
    maxima[...] = jnp.full_like(maxima, -1e30)
    total[...] = jnp.zeros_like(total)
    acc[...] = jnp.zeros_like(acc)

    for weight in weights[:2]:
        weight.wait()
    centre, scale = gather_moments(0)
    gain = scale * attn_gain[...]
    positions = kv[r].reshape(rows, channels).astype(jnp.float32)
    normed = ((positions - centre) * gain + attn_shift[...]).astype(jnp.bfloat16)
    query = jnp.dot(normed, wq[...], preferred_element_type=jnp.float32).astype(jnp.bfloat16)
    folded = lax.dot_general(query, wk[...], NT, preferred_element_type=jnp.float32) * (
        LOG2E / math.sqrt(channels)
    )
    queries[...] = (folded * gain).astype(jnp.bfloat16)
    constant = jnp.sum(folded * (attn_shift[...] - centre * gain), axis=1, keepdims=True)
    bias[...] = jnp.broadcast_to(constant, bias.shape)

    def attend(b, k):
        block = kv[b, k]
        scores = lax.dot_general(queries[...], block, NT, preferred_element_type=jnp.float32)
        scores = scores + jnp.tile(bias[...], (1, chunk // 128))
        newest = jnp.maximum(maxima[...], jnp.max(scores, axis=1, keepdims=True))
        fade = jnp.exp2(maxima[...] - newest)
        maxima[...] = newest
        probs = jnp.exp2(scores - jnp.tile(newest, (1, chunk // 128))).astype(jnp.bfloat16)
        kept = probs.astype(jnp.float32)
        summed = total[...] * fade
        for j in range(chunk // 128):
            summed = summed + kept[:, j * 128 : (j + 1) * 128]
        total[...] = summed
        product = jnp.dot(probs, block, preferred_element_type=jnp.float32)
        acc[...] = acc[...] * jnp.tile(fade, (1, channels // 128)) + product

    def relay(t):
        d = t // chunks
        k = t % chunks
        for way, zb in ((0, z - d), (1, z + d)):
            inside = jnp.logical_and(d > 0, jnp.logical_and(zb >= 0, zb < deep))

            @pl.when(inside)
            def _(way=way, zb=zb):
                arrival(zb * 2 + c, k).wait_recv()

                @pl.when((z < deep - 1) if way == 0 else (z > 0))
                def _():
                    piece(way, zb, k).start()

                piece(2, zb, k).start()

    ahead = jnp.where(jnp.logical_and(z > 0, z < deep - 1), chunks, 0)

    @pl.loop(0, deep * chunks)
    def _(t):
        relay(t + ahead)
        d = t // chunks
        k = t % chunks

        @pl.loop(0, 4)
        def _(j):
            side = j % 2
            other = j // 2
            zb = z + d * (2 * side - 1)
            inside = jnp.logical_and(zb >= 0, zb < deep)

            @pl.when(jnp.logical_and(inside, jnp.logical_or(side == 0, d > 0)))
            def _():
                b = zb * 2 + c + other * (1 - 2 * c)

                @pl.when(other == 1)
                def _():
                    arrival(b, k).wait_recv()

                attend(b, k)

    for weight in weights[2:4]:
        weight.wait()
    denominator = jnp.sum(total[...], axis=1, keepdims=True)
    average = (acc[...] / denominator - centre) * gain + attn_shift[...]
    attended = jnp.dot(
        average.astype(jnp.bfloat16), wv[...], preferred_element_type=jnp.float32
    ).astype(jnp.bfloat16)
    field = (
        kv[r].reshape(rows, channels).astype(jnp.float32)
        + jnp.dot(attended, wo[...], preferred_element_type=jnp.float32)
    ).astype(jnp.bfloat16)
    hidden[...] = field
    share_moments(1, field.astype(jnp.float32))

    up = pltpu.make_async_remote_copy(
        src_ref=hidden.at[pl.ds(0, wide)],
        dst_ref=halo.at[1],
        send_sem=halo_send.at[1],
        recv_sem=halo_recv.at[1],
        device_id=(img, r - 1),
        device_id_type=MESH,
    )
    down = pltpu.make_async_remote_copy(
        src_ref=hidden.at[pl.ds(rows - wide, wide)],
        dst_ref=halo.at[0],
        send_sem=halo_send.at[0],
        recv_sem=halo_recv.at[0],
        device_id=(img, r + 1),
        device_id_type=MESH,
    )

    @pl.when(r > 0)
    def _():
        up.start()

    @pl.when(r < n - 1)
    def _():
        down.start()

    @pl.loop(0, deep * chunks)
    def _(t):
        zb = t // chunks
        k = t % chunks

        @pl.when(jnp.logical_and(z < deep - 1, zb <= z))
        def _():
            piece(0, zb, k).wait_send()

        @pl.when(jnp.logical_and(z > 0, zb >= z))
        def _():
            piece(1, zb, k).wait_send()

        piece(2, zb, k).wait_send()

    for weight in weights[4:]:
        weight.wait()
    centre, scale = gather_moments(1)
    gain = scale * conv_gain[...]

    def activate(values):
        v = (values.astype(jnp.float32) - centre) * gain + conv_shift[...]
        return (v / (1.0 + jnp.exp(-v))).astype(jnp.bfloat16)

    def place(line, values):
        for dy in range(3):
            y = line + 1 - dy
            if 0 <= y < lines:
                stacked[y * wide : (y + 1) * wide, dy * channels : (dy + 1) * channels] = values

    for line in range(lines):
        place(line, activate(hidden[line * wide : (line + 1) * wide]))

    @pl.when(r > 0)
    def _():
        up.wait_send()
        down.wait_recv()
        place(-1, activate(halo[0]))

    @pl.when(r == 0)
    def _():
        place(-1, jnp.zeros((wide, channels), jnp.bfloat16))

    @pl.when(r < n - 1)
    def _():
        down.wait_send()
        up.wait_recv()
        place(lines, activate(halo[1]))

    @pl.when(r == n - 1)
    def _():
        place(lines, jnp.zeros((wide, channels), jnp.bfloat16))

    half = 256
    stores = []
    column = lax.broadcasted_iota(jnp.int32, (rows, half), 0) % wide
    for start in range(0, channels, half):
        cut = slice(start, start + half)

        def taps(dx):
            return jnp.dot(stacked[...], wc[dx, :, cut], preferred_element_type=jnp.float32)

        convolved = taps(1)
        convolved = convolved + jnp.where(column > 0, pltpu.roll(taps(0), 1, 0), 0.0)
        convolved = convolved + jnp.where(
            column < wide - 1, pltpu.roll(taps(2), rows - 1, 0), 0.0
        )
        encoded = hidden[:, cut].astype(jnp.float32) + (convolved + conv_bias[:, cut])
        result[:, cut] = encoded.astype(jnp.bfloat16)
        store = pltpu.make_async_copy(
            result.at[:, cut], out.at[:, cut], store_sem.at[start // half]
        )
        store.start()
        stores.append(store)

    for store in stores:
        store.wait()


def local(n, latent, attn_gain, attn_shift, w_query, w_key, w_value, w_out,
          conv_gain, conv_shift, w_conv, conv_bias):
    height, wide, channels = latent.shape
    rows = height * wide
    chunks = rows // CHUNK
    anywhere = pl.BlockSpec(memory_space=pl.ANY)
    vmem = pl.BlockSpec(memory_space=pltpu.VMEM)
    bf16, f32 = jnp.bfloat16, jnp.float32
    square = pltpu.VMEM((channels, channels), bf16)
    dma = pltpu.SemaphoreType.DMA
    encoded = pl.pallas_call(
        functools.partial(kernel, n, wide),
        out_shape=jax.ShapeDtypeStruct((rows, channels), bf16),
        in_specs=[anywhere] * 6 + [vmem] * 5,
        out_specs=anywhere,
        scratch_shapes=[
            pltpu.VMEM((n, chunks, CHUNK, channels), bf16),
            square, square, square, square,
            pltpu.VMEM((3, 3 * channels, channels), bf16),
            square,
            pltpu.VMEM((2, n, 2, channels), f32),
            pltpu.VMEM((rows, channels), bf16),
            pltpu.VMEM((rows, 128), f32),
            pltpu.VMEM((rows, 128), f32),
            pltpu.VMEM((rows, 128), f32),
            pltpu.VMEM((rows, channels), f32),
            pltpu.VMEM((rows, channels), bf16),
            pltpu.VMEM((2, wide, channels), bf16),
            pltpu.VMEM((rows, 3 * channels), bf16),
            dma((chunks,)),
            dma((13,)),
            dma((3, n // 2, chunks)),
            dma((n, chunks)),
            dma((2, n)),
            dma((2, n)),
            dma((2,)),
            dma((2,)),
            pltpu.VMEM((rows, channels), bf16),
            dma((channels // 256,)),
        ],
        compiler_params=pltpu.CompilerParams(
            collective_id=0, has_side_effects=True, vmem_limit_bytes=56 * 1024 * 1024
        ),
    )(
        latent.reshape(chunks, CHUNK, channels), w_query, w_key, w_value, w_out, w_conv,
        *(v.reshape(1, channels) for v in (attn_gain, attn_shift, conv_gain, conv_shift, conv_bias)),
    )
    return encoded.reshape(height, wide, channels)


def solution(mesh):
    in_specs = (P(("img", "row"), None, None), P(), P(), P(), P(), P(), P(), P(), P(), P(), P())
    out_specs = P(("img", "row"), None, None)
    body = functools.partial(local, mesh.shape["row"])
    return jax.shard_map(body, mesh=mesh, in_specs=in_specs, out_specs=out_specs, check_vma=False)
```

profile of v0, /device:TPU:1, one launch (start us, length us, event | category | flops | bytes accessed | tf_op | source)
XLA Modules:
  0.0 106.1 jit_solution(15345807333106020087)
XLA Ops:
  0.0 104.2 %shard_map.109 = bf16[512,512]{1,0:T(8,128)(2,1)} custom-call(bf16[4,128,512]{2,1,0:T(8,128)(2,1)} %latent.1, bf16[512,512]{1,0:T(8,128)(2,1)} %w_query.1, bf16[512,512]{1,0:T(8,128)(2,1)} %w_key.1, bf16[512,512]{1,0:T(8,128)(2,1)} %w_value.1, bf16[512,512]{1,0:T(8,128)(2,1)} %w_out.1, bf16[3,3,512,512]{3,2,1,0:T(8,128)(2,1)} %w_conv.1, f32[1,512]{1,0:T(1,128)} %bitcast.7, ...), custom_call_target="tpu_custom_call" | custom-call | tf_op jit(solution)/shard_map/pallas_call | solution.py:377
  104.2 1.9 %copy.13 = bf16[4,128,512]{2,1,0:T(8,128)(2,1)} copy(bf16[4,128,512]{2,1,0:T(8,128)(2,1)} %bitcast.6) | data formatting | bytes 1048576
where the time goes:
time: 106 us
  Pallas kernels  104 us (98%)
  local copies, waits for them, and re-layouts  1.87 us (2%)
    pallas_call x1, Pallas kernels, local(): pl.pallas_call(functools.partial(kernel, n, wide), out_shape=jax.ShapeDty...  104 us

commit v1 on v0

--- a/solution.py
+++ b/solution.py
@@ -39,6 +39,8 @@
     chunks, chunk, channels = kv.shape[1:]
     rows = chunks * chunk
     deep = n // 2
+    far = deep // 2
+    half_chunks = chunks // 2
     lines = rows // wide
     size = channels // GROUPS
     img = lax.axis_index("img")
@@ -78,7 +80,7 @@
 
     def piece(way, zb, k):
         b = zb * 2 + c
-        target = (r + 2, r - 2, partner)[way]
+        target = (lax.rem(r + 2, n), lax.rem(r + n - 2, n), partner)[way]
         return pltpu.make_async_remote_copy(
             src_ref=kv.at[b, k],
             dst_ref=kv.at[b, k],
@@ -119,14 +121,8 @@
         )
 
     def send_own(k):
-        @pl.when(z < deep - 1)
-        def _():
-            piece(0, z, k).start()
-
-        @pl.when(z > 0)
-        def _():
-            piece(1, z, k).start()
-
+        piece(0, z, k).start()
+        piece(1, z, k).start()
         piece(2, z, k).start()
 
     def share_moments(which, field):
@@ -205,38 +201,48 @@
         product = jnp.dot(probs, block, preferred_element_type=jnp.float32)
         acc[...] = acc[...] * jnp.tile(fade, (1, channels // 128)) + product
 
+    def split(way, d, k):
+        whole = d < far
+        part = jnp.logical_and(d == far, (k < half_chunks) if way == 0 else (k >= half_chunks))
+        return jnp.logical_or(whole, part)
+
     def relay(t):
         d = t // chunks
         k = t % chunks
-        for way, zb in ((0, z - d), (1, z + d)):
-            inside = jnp.logical_and(d > 0, jnp.logical_and(zb >= 0, zb < deep))
-
-            @pl.when(inside)
+        for way in (0, 1):
+            zb = lax.rem(z + (deep - d if way == 0 else d), deep)
+
+            @pl.when(split(way, d, k))
             def _(way=way, zb=zb):
                 arrival(zb * 2 + c, k).wait_recv()
 
-                @pl.when((z < deep - 1) if way == 0 else (z > 0))
+                @pl.when(split(way, d + 1, k))
                 def _():
                     piece(way, zb, k).start()
 
                 piece(2, zb, k).start()
 
-    ahead = jnp.where(jnp.logical_and(z > 0, z < deep - 1), chunks, 0)
-
-    @pl.loop(0, deep * chunks)
+    @pl.loop(0, (far + 1) * chunks)
     def _(t):
-        relay(t + ahead)
         d = t // chunks
         k = t % chunks
+
+        @pl.when(t < chunks)
+        def _():
+            relay(t + chunks)
+
+        @pl.when(t >= 2 * chunks)
+        def _():
+            relay(t)
 
         @pl.loop(0, 4)
         def _(j):
             side = j % 2
             other = j // 2
-            zb = z + d * (2 * side - 1)
-            inside = jnp.logical_and(zb >= 0, zb < deep)
-
-            @pl.when(jnp.logical_and(inside, jnp.logical_or(side == 0, d > 0)))
+            zb = lax.rem(z + jnp.where(side == 0, deep - d, d), deep)
+            mine = jnp.where(side == 0, split(0, d, k), split(1, d, k))
+
+            @pl.when(jnp.logical_and(mine, jnp.logical_or(side == 0, d > 0)))
             def _():
                 b = zb * 2 + c + other * (1 - 2 * c)
 
@@ -290,11 +296,11 @@
         zb = t // chunks
         k = t % chunks
 
-        @pl.when(jnp.logical_and(z < deep - 1, zb <= z))
+        @pl.when(split(0, lax.rem(z + deep - zb, deep) + 1, k))
         def _():
             piece(0, zb, k).wait_send()
 
-        @pl.when(jnp.logical_and(z > 0, zb >= z))
+        @pl.when(split(1, lax.rem(zb + deep - z, deep) + 1, k))
         def _():
             piece(1, zb, k).wait_send()
 

time: 106 us -> 87.7 us (0.83)
  Pallas kernels: 104 us -> 85.7 us
    pallas_call x1, Pallas kernels: 104 us -> 85.7 us  [local(): pl.pallas_call(functools.partial(kernel, n, wide), out_shape=jax.ShapeDty...]
where the time goes in v1:
time: 87.7 us; the launch traced here: 87.5 us
  Pallas kernels  85.7 us (98%)
  local copies, waits for them, and re-layouts  1.87 us (2%)
    pallas_call x1, Pallas kernels, local(): pl.pallas_call(functools.partial(kernel, n, wide), out_shape=jax.ShapeDty...  85.7 us
    unnamed x1, local copies, waits for them, and re-layouts  1.87 us

profile of v1, /device:TPU:1, one launch (start us, length us, event | category | flops | bytes accessed | tf_op | source)
XLA Modules:
  0.0 87.5 jit_solution(17419912221276272970)
XLA Ops:
  0.0 85.7 %shard_map.109 = bf16[512,512]{1,0:T(8,128)(2,1)} custom-call(bf16[4,128,512]{2,1,0:T(8,128)(2,1)} %latent.1, bf16[512,512]{1,0:T(8,128)(2,1)} %w_query.1, bf16[512,512]{1,0:T(8,128)(2,1)} %w_key.1, bf16[512,512]{1,0:T(8,128)(2,1)} %w_value.1, bf16[512,512]{1,0:T(8,128)(2,1)} %w_out.1, bf16[3,3,512,512]{3,2,1,0:T(8,128)(2,1)} %w_conv.1, f32[1,512]{1,0:T(1,128)} %bitcast.7, ...), custom_call_target="tpu_custom_call" | custom-call | tf_op jit(solution)/shard_map/pallas_call | solution.py:383
  85.7 1.9 %copy.13 = bf16[4,128,512]{2,1,0:T(8,128)(2,1)} copy(bf16[4,128,512]{2,1,0:T(8,128)(2,1)} %bitcast.6) | data formatting | bytes 1048576

commit v2 on v1

--- a/solution.py
+++ b/solution.py
@@ -32,13 +32,12 @@
     latent, w_query, w_key, w_value, w_out, w_conv,
     attn_gain, attn_shift, conv_gain, conv_shift, conv_bias,
     out,
-    kv, wq, wk, wv, wo, wc, ones, moments, queries, bias, maxima, total, acc, hidden, halo, stacked,
+    kv, wq, wk, wv, wo, wvo, wc, ones, moments, queries, bias, maxima, total, acc, hidden, halo, stacked,
     load_sem, weight_sem, send_sem, recv_sem, stat_send, stat_recv, halo_send, halo_recv,
     result, store_sem,
 ):
-    chunks, chunk, channels = kv.shape[1:]
+    deep, chunks, _, chunk, channels = kv.shape
     rows = chunks * chunk
-    deep = n // 2
     far = deep // 2
     half_chunks = chunks // 2
     lines = rows // wide
@@ -50,7 +49,7 @@
     partner = r + 1 - 2 * c
 
     loads = [
-        pltpu.make_async_copy(latent.at[k], kv.at[r, k], load_sem.at[k]) for k in range(chunks)
+        pltpu.make_async_copy(latent.at[k], kv.at[z, k, c], load_sem.at[k]) for k in range(chunks)
     ]
     for load in loads:
         load.start()
@@ -79,23 +78,22 @@
         )
 
     def piece(way, zb, k):
-        b = zb * 2 + c
         target = (lax.rem(r + 2, n), lax.rem(r + n - 2, n), partner)[way]
         return pltpu.make_async_remote_copy(
-            src_ref=kv.at[b, k],
-            dst_ref=kv.at[b, k],
+            src_ref=kv.at[zb, k, c],
+            dst_ref=kv.at[zb, k, c],
             send_sem=send_sem.at[way, zb, k],
-            recv_sem=recv_sem.at[b, k],
+            recv_sem=recv_sem.at[c, zb, k],
             device_id=(img, target),
             device_id_type=MESH,
         )
 
-    def arrival(b, k):
+    def arrival(core, zb, k):
         return pltpu.make_async_remote_copy(
-            src_ref=kv.at[b, k],
-            dst_ref=kv.at[b, k],
+            src_ref=kv.at[zb, k, core],
+            dst_ref=kv.at[zb, k, core],
             send_sem=send_sem.at[0, 0, 0],
-            recv_sem=recv_sem.at[b, k],
+            recv_sem=recv_sem.at[core, zb, k],
             device_id=(img, partner),
             device_id_type=MESH,
         )
@@ -120,6 +118,9 @@
             device_id_type=MESH,
         )
 
+    def own():
+        return kv[z, :, c]
+
     def send_own(k):
         piece(0, z, k).start()
         piece(1, z, k).start()
@@ -160,7 +161,7 @@
         load.wait()
     pl.semaphore_wait(barrier, n - 1)
     send_own(0)
-    share_moments(0, kv[r].reshape(rows, channels).astype(jnp.float32))
+    share_moments(0, own().reshape(rows, channels).astype(jnp.float32))
     for k in range(1, chunks):
         send_own(k)
 
@@ -175,7 +176,7 @@
         weight.wait()
     centre, scale = gather_moments(0)
     gain = scale * attn_gain[...]
-    positions = kv[r].reshape(rows, channels).astype(jnp.float32)
+    positions = own().reshape(rows, channels).astype(jnp.float32)
     normed = ((positions - centre) * gain + attn_shift[...]).astype(jnp.bfloat16)
     query = jnp.dot(normed, wq[...], preferred_element_type=jnp.float32).astype(jnp.bfloat16)
     folded = lax.dot_general(query, wk[...], NT, preferred_element_type=jnp.float32) * (
@@ -185,84 +186,92 @@
     constant = jnp.sum(folded * (attn_shift[...] - centre * gain), axis=1, keepdims=True)
     bias[...] = jnp.broadcast_to(constant, bias.shape)
 
-    def attend(b, k):
-        block = kv[b, k]
-        scores = lax.dot_general(queries[...], block, NT, preferred_element_type=jnp.float32)
-        scores = scores + jnp.tile(bias[...], (1, chunk // 128))
-        newest = jnp.maximum(maxima[...], jnp.max(scores, axis=1, keepdims=True))
-        fade = jnp.exp2(maxima[...] - newest)
-        maxima[...] = newest
-        probs = jnp.exp2(scores - jnp.tile(newest, (1, chunk // 128))).astype(jnp.bfloat16)
-        kept = probs.astype(jnp.float32)
-        summed = total[...] * fade
-        for j in range(chunk // 128):
-            summed = summed + kept[:, j * 128 : (j + 1) * 128]
-        total[...] = summed
-        product = jnp.dot(probs, block, preferred_element_type=jnp.float32)
-        acc[...] = acc[...] * jnp.tile(fade, (1, channels // 128)) + product
-
-    def split(way, d, k):
-        whole = d < far
-        part = jnp.logical_and(d == far, (k < half_chunks) if way == 0 else (k >= half_chunks))
-        return jnp.logical_or(whole, part)
-
-    def relay(t):
-        d = t // chunks
-        k = t % chunks
-        for way in (0, 1):
-            zb = lax.rem(z + (deep - d if way == 0 else d), deep)
-
-            @pl.when(split(way, d, k))
-            def _(way=way, zb=zb):
-                arrival(zb * 2 + c, k).wait_recv()
-
-                @pl.when(split(way, d + 1, k))
-                def _():
-                    piece(way, zb, k).start()
-
-                piece(2, zb, k).start()
-
-    @pl.loop(0, (far + 1) * chunks)
-    def _(t):
-        d = t // chunks
-        k = t % chunks
-
-        @pl.when(t < chunks)
-        def _():
-            relay(t + chunks)
-
-        @pl.when(t >= 2 * chunks)
-        def _():
-            relay(t)
-
-        @pl.loop(0, 4)
-        def _(j):
-            side = j % 2
-            other = j // 2
-            zb = lax.rem(z + jnp.where(side == 0, deep - d, d), deep)
-            mine = jnp.where(side == 0, split(0, d, k), split(1, d, k))
-
-            @pl.when(jnp.logical_and(mine, jnp.logical_or(side == 0, d > 0)))
-            def _():
-                b = zb * 2 + c + other * (1 - 2 * c)
-
-                @pl.when(other == 1)
-                def _():
-                    arrival(b, k).wait_recv()
-
-                attend(b, k)
-
     for weight in weights[2:4]:
         weight.wait()
+    wvo[...] = jnp.dot(wv[...], wo[...], preferred_element_type=jnp.float32).astype(jnp.bfloat16)
+
+    lanes = 128
+    halves = [slice(i, i + rows // 2) for i in range(0, rows, rows // 2)]
+
+    def attend(places):
+        blocks = [kv[zb, k].reshape(2 * chunk, channels) for zb, k in places]
+        scores = [
+            [
+                lax.dot_general(queries[part], block, NT, preferred_element_type=jnp.float32)
+                for block in blocks
+            ]
+            for part in halves
+        ]
+        for part, pair in zip(halves, scores):
+            columns = [
+                score[:, j : j + lanes] for score in pair for j in range(0, 2 * chunk, lanes)
+            ]
+            peak = functools.reduce(jnp.maximum, columns)
+            offset = bias[part]
+            newest = jnp.maximum(maxima[part], jnp.max(peak, axis=1, keepdims=True) + offset)
+            fade = jnp.exp2(maxima[part] - newest)
+            maxima[part] = newest
+            level = newest - offset
+            weights = [jnp.exp2(column - level) for column in columns]
+            total[part] = functools.reduce(jnp.add, weights, total[part] * fade)
+            each = len(weights) // 2
+            product = 0.0
+            for i, block in enumerate(blocks):
+                probs = jnp.concatenate(weights[i * each : (i + 1) * each], axis=1)
+                product = product + jnp.dot(
+                    probs.astype(jnp.bfloat16), block, preferred_element_type=jnp.float32
+                )
+            acc[part] = acc[part] * jnp.tile(fade, (1, channels // lanes)) + product
+
+    def split(way, d, k):
+        part = (k < half_chunks) if way == 0 else (k >= half_chunks)
+        return jnp.logical_or(d < far, jnp.logical_and(d == far, part))
+
+    own_steps = half_chunks
+
+    def spot(way, s):
+        e = s - own_steps
+        d = jnp.where(e < 0, 0, e // chunks + 1)
+        last = d == far
+        step = jnp.where(e < 0, 2 * s + way, lax.rem(e + chunks, chunks) + jnp.where(last, way * half_chunks, 0))
+        zb = lax.rem(z + (deep - d if way == 0 else d), deep)
+        return d, zb, step
+
+    def relay(s):
+        for way in (0, 1):
+            d, zb, k = spot(way, s)
+            arrival(c, zb, k).wait_recv()
+
+            @pl.when(split(way, d + 1, k))
+            def _(way=way, zb=zb, k=k):
+                piece(way, zb, k).start()
+
+            piece(2, zb, k).start()
+
+    ahead = 2
+    steps = own_steps + (far - 1) * chunks + half_chunks
+    for s in range(own_steps, own_steps + ahead):
+        relay(s)
+
+    @pl.loop(0, steps)
+    def _(s):
+        @pl.when(s >= own_steps + ahead)
+        def _():
+            relay(s)
+
+        places = []
+        for way in (0, 1):
+            d, zb, k = spot(way, s)
+            arrival(1 - c, zb, k).wait_recv()
+            places.append((zb, k))
+        attend(places)
+
     denominator = jnp.sum(total[...], axis=1, keepdims=True)
-    average = (acc[...] / denominator - centre) * gain + attn_shift[...]
+    average = (acc[...] * (1.0 / denominator) - centre) * gain + attn_shift[...]
     attended = jnp.dot(
-        average.astype(jnp.bfloat16), wv[...], preferred_element_type=jnp.float32
-    ).astype(jnp.bfloat16)
-    field = (
-        kv[r].reshape(rows, channels).astype(jnp.float32)
-        + jnp.dot(attended, wo[...], preferred_element_type=jnp.float32)
-    ).astype(jnp.bfloat16)
+        average.astype(jnp.bfloat16), wvo[...], preferred_element_type=jnp.float32
+    )
+    field = (own().reshape(rows, channels).astype(jnp.float32) + attended).astype(jnp.bfloat16)
     hidden[...] = field
     share_moments(1, field.astype(jnp.float32))
 
@@ -386,8 +395,8 @@
         in_specs=[anywhere] * 6 + [vmem] * 5,
         out_specs=anywhere,
         scratch_shapes=[
-            pltpu.VMEM((n, chunks, CHUNK, channels), bf16),
-            square, square, square, square,
+            pltpu.VMEM((n // 2, chunks, 2, CHUNK, channels), bf16),
+            square, square, square, square, square,
             pltpu.VMEM((3, 3 * channels, channels), bf16),
             square,
             pltpu.VMEM((2, n, 2, channels), f32),
@@ -402,7 +411,7 @@
             dma((chunks,)),
             dma((13,)),
             dma((3, n // 2, chunks)),
-            dma((n, chunks)),
+            dma((2, n // 2, chunks)),
             dma((2, n)),
             dma((2, n)),
             dma((2,)),

time: 87.7 us -> 69.4 us (0.79)
  Pallas kernels: 85.7 us -> 67.3 us
    pallas_call x1, Pallas kernels: 85.7 us -> 67.3 us  [local(): pl.pallas_call(functools.partial(kernel, n, wide), out_shape=jax.ShapeDty...]
where the time goes in v2:
time: 69.4 us; the launch traced here: 69.2 us
  Pallas kernels  67.3 us (97%)
  local copies, waits for them, and re-layouts  1.87 us (3%)
    pallas_call x1, Pallas kernels, local(): pl.pallas_call(functools.partial(kernel, n, wide), out_shape=jax.ShapeDty...  67.3 us
    unnamed x1, local copies, waits for them, and re-layouts  1.87 us

profile of v2, /device:TPU:1, one launch (start us, length us, event | category | flops | bytes accessed | tf_op | source)
XLA Modules:
  0.0 69.2 jit_solution(5324225316477314631)
XLA Ops:
  0.0 67.3 %shard_map.109 = bf16[512,512]{1,0:T(8,128)(2,1)} custom-call(bf16[4,128,512]{2,1,0:T(8,128)(2,1)} %latent.1, bf16[512,512]{1,0:T(8,128)(2,1)} %w_query.1, bf16[512,512]{1,0:T(8,128)(2,1)} %w_key.1, bf16[512,512]{1,0:T(8,128)(2,1)} %w_value.1, bf16[512,512]{1,0:T(8,128)(2,1)} %w_out.1, bf16[3,3,512,512]{3,2,1,0:T(8,128)(2,1)} %w_conv.1, f32[1,512]{1,0:T(1,128)} %bitcast.7, ...), custom_call_target="tpu_custom_call" | custom-call | tf_op jit(solution)/shard_map/pallas_call | solution.py:392
  67.3 1.9 %copy.13 = bf16[4,128,512]{2,1,0:T(8,128)(2,1)} copy(bf16[4,128,512]{2,1,0:T(8,128)(2,1)} %bitcast.6) | data formatting | bytes 1048576

commit v3 on v2

--- a/solution.py
+++ b/solution.py
@@ -30,16 +30,17 @@
 def kernel(
     n, wide,
     latent, w_query, w_key, w_value, w_out, w_conv,
-    attn_gain, attn_shift, conv_gain, conv_shift, conv_bias,
+    attn_gain_in, attn_shift_in, conv_gain_in, conv_shift_in, conv_bias_in,
     out,
     kv, wq, wk, wv, wo, wvo, wc, ones, moments, queries, bias, maxima, total, acc, hidden, halo, stacked,
     load_sem, weight_sem, send_sem, recv_sem, stat_send, stat_recv, halo_send, halo_recv,
-    result, store_sem,
+    result, store_sem, vectors, vector_sem, entered,
 ):
     deep, chunks, _, chunk, channels = kv.shape
     rows = chunks * chunk
     far = deep // 2
     half_chunks = chunks // 2
+    early = 2
     lines = rows // wide
     size = channels // GROUPS
     img = lax.axis_index("img")
@@ -47,6 +48,12 @@
     z = r // 2
     c = r % 2
     partner = r + 1 - 2 * c
+
+    barrier = pltpu.get_barrier_semaphore()
+
+    upward, downward = lax.rem(r + 2, n), lax.rem(r + n - 2, n)
+    for target in (upward, downward, partner):
+        pl.semaphore_signal(barrier, inc=1, device_id=(img, target), device_id_type=MESH)
 
     loads = [
         pltpu.make_async_copy(latent.at[k], kv.at[z, k, c], load_sem.at[k]) for k in range(chunks)
@@ -69,16 +76,17 @@
     for weight in weights:
         weight.start()
 
-    barrier = pltpu.get_barrier_semaphore()
-
-    @pl.loop(1, n)
-    def _(j):
-        pl.semaphore_signal(
-            barrier, inc=1, device_id=(img, lax.rem(r + j, n)), device_id_type=MESH
-        )
+    small = [
+        pltpu.make_async_copy(source, vectors.at[pl.ds(i, 1)], vector_sem.at[i])
+        for i, source in enumerate(
+            [attn_gain_in, attn_shift_in, conv_gain_in, conv_shift_in, conv_bias_in]
+        )
+    ]
+    for copy in small:
+        copy.start()
 
     def piece(way, zb, k):
-        target = (lax.rem(r + 2, n), lax.rem(r + n - 2, n), partner)[way]
+        target = (upward, downward, partner)[way]
         return pltpu.make_async_remote_copy(
             src_ref=kv.at[zb, k, c],
             dst_ref=kv.at[zb, k, c],
@@ -157,12 +165,21 @@
         variance = spread_groups(whole, ones[...]) * (1.0 / (n * size * rows))
         return centre, lax.rsqrt(variance + EPS)
 
-    for load in loads:
-        load.wait()
-    pl.semaphore_wait(barrier, n - 1)
-    send_own(0)
+    pl.semaphore_wait(barrier, 3)
+    for k in range(chunks):
+        loads[k].wait()
+        if k < early:
+            send_own(k)
+    for j in range(far - 1):
+        for target in (upward, downward):
+            pl.semaphore_signal(
+                entered.at[j], inc=1, device_id=(img, target), device_id_type=MESH
+            )
+        pl.semaphore_wait(entered.at[j], 2)
+    pl.semaphore_signal(entered.at[far - 1], inc=1, device_id=(img, partner), device_id_type=MESH)
+    pl.semaphore_wait(entered.at[far - 1], 1)
     share_moments(0, own().reshape(rows, channels).astype(jnp.float32))
-    for k in range(1, chunks):
+    for k in range(early, chunks):
         send_own(k)
 
     left_group = lax.broadcasted_iota(jnp.int32, (channels, channels), 0) // size
@@ -174,16 +191,20 @@
 
     for weight in weights[:2]:
         weight.wait()
+    for copy in small:
+        copy.wait()
+    attn_gain, attn_shift, conv_gain, conv_shift = (vectors[i : i + 1] for i in range(4))
+    conv_bias = vectors.at[4:5]
     centre, scale = gather_moments(0)
-    gain = scale * attn_gain[...]
+    gain = scale * attn_gain
     positions = own().reshape(rows, channels).astype(jnp.float32)
-    normed = ((positions - centre) * gain + attn_shift[...]).astype(jnp.bfloat16)
+    normed = ((positions - centre) * gain + attn_shift).astype(jnp.bfloat16)
     query = jnp.dot(normed, wq[...], preferred_element_type=jnp.float32).astype(jnp.bfloat16)
     folded = lax.dot_general(query, wk[...], NT, preferred_element_type=jnp.float32) * (
         LOG2E / math.sqrt(channels)
     )
     queries[...] = (folded * gain).astype(jnp.bfloat16)
-    constant = jnp.sum(folded * (attn_shift[...] - centre * gain), axis=1, keepdims=True)
+    constant = jnp.sum(folded * (attn_shift - centre * gain), axis=1, keepdims=True)
     bias[...] = jnp.broadcast_to(constant, bias.shape)
 
     for weight in weights[2:4]:
@@ -267,7 +288,7 @@
         attend(places)
 
     denominator = jnp.sum(total[...], axis=1, keepdims=True)
-    average = (acc[...] * (1.0 / denominator) - centre) * gain + attn_shift[...]
+    average = (acc[...] * (1.0 / denominator) - centre) * gain + attn_shift
     attended = jnp.dot(
         average.astype(jnp.bfloat16), wvo[...], preferred_element_type=jnp.float32
     )
@@ -318,10 +339,10 @@
     for weight in weights[4:]:
         weight.wait()
     centre, scale = gather_moments(1)
-    gain = scale * conv_gain[...]
+    gain = scale * conv_gain
 
     def activate(values):
-        v = (values.astype(jnp.float32) - centre) * gain + conv_shift[...]
+        v = (values.astype(jnp.float32) - centre) * gain + conv_shift
         return (v / (1.0 + jnp.exp(-v))).astype(jnp.bfloat16)
 
     def place(line, values):
@@ -385,14 +406,13 @@
     rows = height * wide
     chunks = rows // CHUNK
     anywhere = pl.BlockSpec(memory_space=pl.ANY)
-    vmem = pl.BlockSpec(memory_space=pltpu.VMEM)
     bf16, f32 = jnp.bfloat16, jnp.float32
     square = pltpu.VMEM((channels, channels), bf16)
     dma = pltpu.SemaphoreType.DMA
     encoded = pl.pallas_call(
         functools.partial(kernel, n, wide),
         out_shape=jax.ShapeDtypeStruct((rows, channels), bf16),
-        in_specs=[anywhere] * 6 + [vmem] * 5,
+        in_specs=[anywhere] * 11,
         out_specs=anywhere,
         scratch_shapes=[
             pltpu.VMEM((n // 2, chunks, 2, CHUNK, channels), bf16),
@@ -418,6 +438,9 @@
             dma((2,)),
             pltpu.VMEM((rows, channels), bf16),
             dma((channels // 256,)),
+            pltpu.VMEM((8, channels), f32),
+            dma((5,)),
+            pltpu.SemaphoreType.REGULAR((n // 4,)),
         ],
         compiler_params=pltpu.CompilerParams(
             collective_id=0, has_side_effects=True, vmem_limit_bytes=56 * 1024 * 1024

time: 69.4 us -> 67.4 us (0.971)
  Pallas kernels: 67.3 us -> 65.4 us
    pallas_call x1, Pallas kernels: 67.3 us -> 65.4 us  [local(): pl.pallas_call(functools.partial(kernel, n, wide), out_shape=jax.ShapeDty...]
where the time goes in v3:
time: 67.4 us; the launch traced here: 67.3 us
  Pallas kernels  65.4 us (97%)
  local copies, waits for them, and re-layouts  1.87 us (3%)
    pallas_call x1, Pallas kernels, local(): pl.pallas_call(functools.partial(kernel, n, wide), out_shape=jax.ShapeDty...  65.4 us
    unnamed x1, local copies, waits for them, and re-layouts  1.87 us

profile of v3, /device:TPU:1, one launch (start us, length us, event | category | flops | bytes accessed | tf_op | source)
XLA Modules:
  0.0 67.3 jit_solution(16531151759114885508)
XLA Ops:
  0.0 65.4 %shard_map.109 = bf16[512,512]{1,0:T(8,128)(2,1)} custom-call(bf16[4,128,512]{2,1,0:T(8,128)(2,1)} %latent.1, bf16[512,512]{1,0:T(8,128)(2,1)} %w_query.1, bf16[512,512]{1,0:T(8,128)(2,1)} %w_key.1, bf16[512,512]{1,0:T(8,128)(2,1)} %w_value.1, bf16[512,512]{1,0:T(8,128)(2,1)} %w_out.1, bf16[3,3,512,512]{3,2,1,0:T(8,128)(2,1)} %w_conv.1, f32[1,512]{1,0:T(1,128)} %bitcast.7, ...), custom_call_target="tpu_custom_call" | custom-call | tf_op jit(solution)/shard_map/pallas_call | solution.py:412
  65.4 1.9 %copy.13 = bf16[4,128,512]{2,1,0:T(8,128)(2,1)} copy(bf16[4,128,512]{2,1,0:T(8,128)(2,1)} %bitcast.6) | data formatting | bytes 1048576

commit v4 on v3

--- a/solution.py
+++ b/solution.py
@@ -16,15 +16,20 @@
 NT = (((1,), (1,)), ((), ()))
 
 
-def spread_groups(row, ones):
-    high = row.astype(jnp.bfloat16).astype(jnp.float32)
-    rest = row - high
-    mid = rest.astype(jnp.bfloat16).astype(jnp.float32)
-    low = rest - mid
-    index = lax.broadcasted_iota(jnp.int32, (16, row.shape[1]), 0)
-    parts = jnp.where(index == 0, high, jnp.where(index == 1, mid, jnp.where(index == 2, low, 0.0)))
-    sums = jnp.dot(parts.astype(jnp.bfloat16), ones, preferred_element_type=jnp.float32)
-    return jnp.sum(sums, axis=0, keepdims=True)
+def exact_dot(vectors, matrix):
+    index = lax.broadcasted_iota(jnp.int32, (16, vectors[0].shape[1]), 0)
+    parts = jnp.zeros(index.shape, jnp.float32)
+    for i, vector in enumerate(vectors):
+        high = vector.astype(jnp.bfloat16).astype(jnp.float32)
+        rest = vector - high
+        mid = rest.astype(jnp.bfloat16).astype(jnp.float32)
+        for j, part in enumerate((high, mid, rest - mid)):
+            parts = jnp.where(index == 3 * i + j, part, parts)
+    sums = jnp.dot(parts.astype(jnp.bfloat16), matrix, preferred_element_type=jnp.float32)
+    return [
+        sums[3 * i : 3 * i + 1] + sums[3 * i + 1 : 3 * i + 2] + sums[3 * i + 2 : 3 * i + 3]
+        for i in range(len(vectors))
+    ]
 
 
 def kernel(
@@ -32,7 +37,7 @@
     latent, w_query, w_key, w_value, w_out, w_conv,
     attn_gain_in, attn_shift_in, conv_gain_in, conv_shift_in, conv_bias_in,
     out,
-    kv, wq, wk, wv, wo, wvo, wc, ones, moments, queries, bias, maxima, total, acc, hidden, halo, stacked,
+    kv, wq, wk, wv, wo, wvo, wc, ones, fold, spread, moments, queries, bias, maxima, total, acc, hidden, halo, stacked,
     load_sem, weight_sem, send_sem, recv_sem, stat_send, stat_recv, halo_send, halo_recv,
     result, store_sem, vectors, vector_sem, entered,
 ):
@@ -134,12 +139,40 @@
         piece(1, z, k).start()
         piece(2, z, k).start()
 
+    def split(way, d, k):
+        part = (k < half_chunks) if way == 0 else (k >= half_chunks)
+        return jnp.logical_or(d < far, jnp.logical_and(d == far, part))
+
+    own_steps = half_chunks
+
+    def spot(way, s):
+        e = s - own_steps
+        d = jnp.where(e < 0, 0, e // chunks + 1)
+        last = d == far
+        step = jnp.where(e < 0, 2 * s + way, lax.rem(e + chunks, chunks) + jnp.where(last, way * half_chunks, 0))
+        zb = lax.rem(z + (deep - d if way == 0 else d), deep)
+        return d, zb, step
+
+    def relay(s):
+        for way in (0, 1):
+            d, zb, k = spot(way, s)
+            arrival(c, zb, k).wait_recv()
+
+            @pl.when(split(way, d + 1, k))
+            def _(way=way, zb=zb, k=k):
+                piece(way, zb, k).start()
+
+            piece(2, zb, k).start()
+
     def share_moments(which, field):
         mean = jnp.sum(field, axis=0, keepdims=True) * (1.0 / rows)
         offset = field - mean
         square = jnp.sum(offset * offset, axis=0, keepdims=True)
-        moments[which, r, 0:1, :] = mean
-        moments[which, r, 1:2, :] = square
+        (near,) = exact_dot([mean], ones[...])
+        away = mean - near * (1.0 / size)
+        sums, squares = exact_dot([mean, square + rows * (away * away)], fold[...])
+        moments[which, r, 0:1, :] = sums * (1.0 / size)
+        moments[which, r, 1:2, :] = squares
 
         @pl.loop(1, n)
         def _(j):
@@ -157,13 +190,22 @@
         every = moments[which]
         means = every[:, 0, :]
         squares = every[:, 1, :]
-        centre = spread_groups(jnp.sum(means, axis=0, keepdims=True), ones[...]) * (
-            1.0 / (n * size)
-        )
+        centre = jnp.sum(means, axis=0, keepdims=True) * (1.0 / n)
         away = means - centre
-        whole = jnp.sum(squares + rows * (away * away), axis=0, keepdims=True)
-        variance = spread_groups(whole, ones[...]) * (1.0 / (n * size * rows))
-        return centre, lax.rsqrt(variance + EPS)
+        whole = jnp.sum(squares + (rows * size) * (away * away), axis=0, keepdims=True)
+        scale = lax.rsqrt(whole * (1.0 / (n * size * rows)) + EPS)
+        return exact_dot([centre, scale], spread[...])
+
+    def groups(shape, left, right):
+        rows_of, columns_of = (lax.broadcasted_iota(jnp.int32, shape, i) for i in (0, 1))
+        return jnp.where(rows_of // left == columns_of // right, 1.0, 0.0).astype(jnp.bfloat16)
+
+    ones[...] = groups(ones.shape, size, size)
+    fold[...] = groups(fold.shape, size, 1)
+    spread[...] = groups(spread.shape, 1, size)
+    maxima[...] = jnp.full_like(maxima, -1e30)
+    total[...] = jnp.zeros_like(total)
+    acc[...] = jnp.zeros_like(acc)
 
     pl.semaphore_wait(barrier, 3)
     for k in range(chunks):
@@ -182,12 +224,8 @@
     for k in range(early, chunks):
         send_own(k)
 
-    left_group = lax.broadcasted_iota(jnp.int32, (channels, channels), 0) // size
-    right_group = lax.broadcasted_iota(jnp.int32, (channels, channels), 1) // size
-    ones[...] = jnp.where(left_group == right_group, 1.0, 0.0).astype(jnp.bfloat16)
-    maxima[...] = jnp.full_like(maxima, -1e30)
-    total[...] = jnp.zeros_like(total)
-    acc[...] = jnp.zeros_like(acc)
+    for s in (own_steps, own_steps + 1):
+        relay(s)
 
     for weight in weights[:2]:
         weight.wait()
@@ -214,8 +252,7 @@
     lanes = 128
     halves = [slice(i, i + rows // 2) for i in range(0, rows, rows // 2)]
 
-    def attend(places):
-        blocks = [kv[zb, k].reshape(2 * chunk, channels) for zb, k in places]
+    def attend(blocks):
         scores = [
             [
                 lax.dot_general(queries[part], block, NT, preferred_element_type=jnp.float32)
@@ -235,7 +272,7 @@
             level = newest - offset
             weights = [jnp.exp2(column - level) for column in columns]
             total[part] = functools.reduce(jnp.add, weights, total[part] * fade)
-            each = len(weights) // 2
+            each = len(weights) // len(blocks)
             product = 0.0
             for i, block in enumerate(blocks):
                 probs = jnp.concatenate(weights[i * each : (i + 1) * each], axis=1)
@@ -244,48 +281,34 @@
                 )
             acc[part] = acc[part] * jnp.tile(fade, (1, channels // lanes)) + product
 
-    def split(way, d, k):
-        part = (k < half_chunks) if way == 0 else (k >= half_chunks)
-        return jnp.logical_or(d < far, jnp.logical_and(d == far, part))
-
-    own_steps = half_chunks
-
-    def spot(way, s):
-        e = s - own_steps
-        d = jnp.where(e < 0, 0, e // chunks + 1)
-        last = d == far
-        step = jnp.where(e < 0, 2 * s + way, lax.rem(e + chunks, chunks) + jnp.where(last, way * half_chunks, 0))
-        zb = lax.rem(z + (deep - d if way == 0 else d), deep)
-        return d, zb, step
-
-    def relay(s):
-        for way in (0, 1):
-            d, zb, k = spot(way, s)
-            arrival(c, zb, k).wait_recv()
-
-            @pl.when(split(way, d + 1, k))
-            def _(way=way, zb=zb, k=k):
-                piece(way, zb, k).start()
-
-            piece(2, zb, k).start()
-
-    ahead = 2
+    relay(own_steps + 2)
     steps = own_steps + (far - 1) * chunks + half_chunks
-    for s in range(own_steps, own_steps + ahead):
-        relay(s)
-
-    @pl.loop(0, steps)
+    lead = 2
+    taper = 6
+
+    @pl.loop(0, steps - 1)
     def _(s):
-        @pl.when(s >= own_steps + ahead)
+        @pl.when(jnp.logical_and(s >= 3, s < taper))
+        def _():
+            relay(s + lead)
+
+        @pl.when(s >= taper + lead)
         def _():
             relay(s)
 
-        places = []
+        blocks = []
         for way in (0, 1):
             d, zb, k = spot(way, s)
             arrival(1 - c, zb, k).wait_recv()
-            places.append((zb, k))
-        attend(places)
+            blocks.append(kv[zb, k].reshape(2 * chunk, channels))
+        attend(blocks)
+
+    final = [spot(way, steps - 1) for way in (0, 1)]
+    relay(steps - 1)
+    attend([jnp.concatenate([kv[zb, k, c] for d, zb, k in final], axis=0)])
+    for d, zb, k in final:
+        arrival(1 - c, zb, k).wait_recv()
+    attend([jnp.concatenate([kv[zb, k, 1 - c] for d, zb, k in final], axis=0)])
 
     denominator = jnp.sum(total[...], axis=1, keepdims=True)
     average = (acc[...] * (1.0 / denominator) - centre) * gain + attn_shift
@@ -345,14 +368,41 @@
         v = (values.astype(jnp.float32) - centre) * gain + conv_shift
         return (v / (1.0 + jnp.exp(-v))).astype(jnp.bfloat16)
 
+    order = [*range(1, lines - 1), 0, lines - 1]
+
     def place(line, values):
         for dy in range(3):
             y = line + 1 - dy
             if 0 <= y < lines:
-                stacked[y * wide : (y + 1) * wide, dy * channels : (dy + 1) * channels] = values
+                slot = order.index(y) * wide
+                stacked[slot : slot + wide, dy * channels : (dy + 1) * channels] = values
+
+    def convolve(first, last):
+        count = (last - first) * wide
+        window = stacked[first * wide : last * wide]
+        column = lax.broadcasted_iota(jnp.int32, (count, channels), 0) % wide
+
+        def taps(dx):
+            return jnp.dot(window, wc[dx], preferred_element_type=jnp.float32)
+
+        convolved = taps(1) + conv_bias[...]
+        convolved = convolved + jnp.where(column > 0, pltpu.roll(taps(0), 1, 0), 0.0)
+        convolved = convolved + jnp.where(
+            column < wide - 1, pltpu.roll(taps(2), count - 1, 0), 0.0
+        )
+        stores = []
+        for i, y in enumerate(order[first:last]):
+            line = slice(y * wide, (y + 1) * wide)
+            part = convolved[i * wide : (i + 1) * wide]
+            result[line] = (hidden[line].astype(jnp.float32) + part).astype(jnp.bfloat16)
+            store = pltpu.make_async_copy(result.at[line], out.at[line], store_sem.at[y])
+            store.start()
+            stores.append(store)
+        return stores
 
     for line in range(lines):
         place(line, activate(hidden[line * wide : (line + 1) * wide]))
+    stores = convolve(0, lines - 2)
 
     @pl.when(r > 0)
     def _():
@@ -374,28 +424,7 @@
     def _():
         place(lines, jnp.zeros((wide, channels), jnp.bfloat16))
 
-    half = 256
-    stores = []
-    column = lax.broadcasted_iota(jnp.int32, (rows, half), 0) % wide
-    for start in range(0, channels, half):
-        cut = slice(start, start + half)
-
-        def taps(dx):
-            return jnp.dot(stacked[...], wc[dx, :, cut], preferred_element_type=jnp.float32)
-
-        convolved = taps(1)
-        convolved = convolved + jnp.where(column > 0, pltpu.roll(taps(0), 1, 0), 0.0)
-        convolved = convolved + jnp.where(
-            column < wide - 1, pltpu.roll(taps(2), rows - 1, 0), 0.0
-        )
-        encoded = hidden[:, cut].astype(jnp.float32) + (convolved + conv_bias[:, cut])
-        result[:, cut] = encoded.astype(jnp.bfloat16)
-        store = pltpu.make_async_copy(
-            result.at[:, cut], out.at[:, cut], store_sem.at[start // half]
-        )
-        store.start()
-        stores.append(store)
-
+    stores += convolve(lines - 2, lines)
     for store in stores:
         store.wait()
 
@@ -419,7 +448,9 @@
             square, square, square, square, square,
             pltpu.VMEM((3, 3 * channels, channels), bf16),
             square,
-            pltpu.VMEM((2, n, 2, channels), f32),
+            pltpu.VMEM((channels, 128), bf16),
+            pltpu.VMEM((128, channels), bf16),
+            pltpu.VMEM((2, n, 2, 128), f32),
             pltpu.VMEM((rows, channels), bf16),
             pltpu.VMEM((rows, 128), f32),
             pltpu.VMEM((rows, 128), f32),
@@ -437,7 +468,7 @@
             dma((2,)),
             dma((2,)),
             pltpu.VMEM((rows, channels), bf16),
-            dma((channels // 256,)),
+            dma((height,)),
             pltpu.VMEM((8, channels), f32),
             dma((5,)),
             pltpu.SemaphoreType.REGULAR((n // 4,)),

time: 67.4 us -> 65.8 us (0.976)
  Pallas kernels: 65.4 us -> 63.8 us
    pallas_call x1, Pallas kernels: 65.4 us -> 63.8 us  [local(): pl.pallas_call(functools.partial(kernel, n, wide), out_shape=jax.ShapeDty...]
where the time goes in v4:
time: 65.8 us; the launch traced here: 65.7 us
  Pallas kernels  63.8 us (97%)
  local copies, waits for them, and re-layouts  1.87 us (3%)
    pallas_call x1, Pallas kernels, local(): pl.pallas_call(functools.partial(kernel, n, wide), out_shape=jax.ShapeDty...  63.8 us
    unnamed x1, local copies, waits for them, and re-layouts  1.87 us

profile of v4, /device:TPU:1, one launch (start us, length us, event | category | flops | bytes accessed | tf_op | source)
XLA Modules:
  0.0 65.7 jit_solution(8062929463973731552)
XLA Ops:
  0.0 63.8 %shard_map.109 = bf16[512,512]{1,0:T(8,128)(2,1)} custom-call(bf16[4,128,512]{2,1,0:T(8,128)(2,1)} %latent.1, bf16[512,512]{1,0:T(8,128)(2,1)} %w_query.1, bf16[512,512]{1,0:T(8,128)(2,1)} %w_key.1, bf16[512,512]{1,0:T(8,128)(2,1)} %w_value.1, bf16[512,512]{1,0:T(8,128)(2,1)} %w_out.1, bf16[3,3,512,512]{3,2,1,0:T(8,128)(2,1)} %w_conv.1, f32[1,512]{1,0:T(1,128)} %bitcast.7, ...), custom_call_target="tpu_custom_call" | custom-call | tf_op jit(solution)/shard_map/pallas_call | solution.py:441
  63.8 1.9 %copy.13 = bf16[4,128,512]{2,1,0:T(8,128)(2,1)} copy(bf16[4,128,512]{2,1,0:T(8,128)(2,1)} %bitcast.6) | data formatting | bytes 1048576

commit v5 on v4

--- a/solution.py
+++ b/solution.py
@@ -39,13 +39,15 @@
     out,
     kv, wq, wk, wv, wo, wvo, wc, ones, fold, spread, moments, queries, bias, maxima, total, acc, hidden, halo, stacked,
     load_sem, weight_sem, send_sem, recv_sem, stat_send, stat_recv, halo_send, halo_recv,
-    result, store_sem, vectors, vector_sem, entered,
+    vectors, vector_sem, entered,
 ):
     deep, chunks, _, chunk, channels = kv.shape
     rows = chunks * chunk
     far = deep // 2
     half_chunks = chunks // 2
-    early = 2
+    early = 3
+    primed = 3
+    lead = 3
     lines = rows // wide
     size = channels // GROUPS
     img = lax.axis_index("img")
@@ -183,10 +185,6 @@
         def _(j):
             stat_arrival(which, lax.rem(r + j, n)).wait_recv()
 
-        @pl.loop(1, n)
-        def _(j):
-            stat_copy(which, j).wait_send()
-
         every = moments[which]
         means = every[:, 0, :]
         squares = every[:, 1, :]
@@ -196,27 +194,32 @@
         scale = lax.rsqrt(whole * (1.0 / (n * size * rows)) + EPS)
         return exact_dot([centre, scale], spread[...])
 
-    def groups(shape, left, right):
-        rows_of, columns_of = (lax.broadcasted_iota(jnp.int32, shape, i) for i in (0, 1))
-        return jnp.where(rows_of // left == columns_of // right, 1.0, 0.0).astype(jnp.bfloat16)
-
-    ones[...] = groups(ones.shape, size, size)
-    fold[...] = groups(fold.shape, size, 1)
-    spread[...] = groups(spread.shape, 1, size)
-    maxima[...] = jnp.full_like(maxima, -1e30)
-    total[...] = jnp.zeros_like(total)
-    acc[...] = jnp.zeros_like(acc)
-
     pl.semaphore_wait(barrier, 3)
     for k in range(chunks):
         loads[k].wait()
         if k < early:
             send_own(k)
+    def groups(shape, left, right):
+        rows_of, columns_of = (lax.broadcasted_iota(jnp.int32, shape, i) for i in (0, 1))
+        return jnp.where(rows_of // left == columns_of // right, 1.0, 0.0).astype(jnp.bfloat16)
+
+    def prepare(j):
+        if j == 0:
+            ones[...] = groups(ones.shape, size, size)
+        if j == 1:
+            fold[...] = groups(fold.shape, size, 1)
+            spread[...] = groups(spread.shape, 1, size)
+            maxima[...] = jnp.full_like(maxima, -1e30)
+            total[...] = jnp.zeros_like(total)
+        if j == 2:
+            acc[...] = jnp.zeros_like(acc)
+
     for j in range(far - 1):
         for target in (upward, downward):
             pl.semaphore_signal(
                 entered.at[j], inc=1, device_id=(img, target), device_id_type=MESH
             )
+        prepare(j)
         pl.semaphore_wait(entered.at[j], 2)
     pl.semaphore_signal(entered.at[far - 1], inc=1, device_id=(img, partner), device_id_type=MESH)
     pl.semaphore_wait(entered.at[far - 1], 1)
@@ -224,7 +227,7 @@
     for k in range(early, chunks):
         send_own(k)
 
-    for s in (own_steps, own_steps + 1):
+    for s in range(own_steps, own_steps + primed):
         relay(s)
 
     for weight in weights[:2]:
@@ -281,14 +284,13 @@
                 )
             acc[part] = acc[part] * jnp.tile(fade, (1, channels // lanes)) + product
 
-    relay(own_steps + 2)
     steps = own_steps + (far - 1) * chunks + half_chunks
-    lead = 2
-    taper = 6
+    first = own_steps + primed - lead
+    taper = first + 3
 
     @pl.loop(0, steps - 1)
     def _(s):
-        @pl.when(jnp.logical_and(s >= 3, s < taper))
+        @pl.when(jnp.logical_and(s >= first, s < taper))
         def _():
             relay(s + lead)
 
@@ -390,19 +392,14 @@
         convolved = convolved + jnp.where(
             column < wide - 1, pltpu.roll(taps(2), count - 1, 0), 0.0
         )
-        stores = []
         for i, y in enumerate(order[first:last]):
             line = slice(y * wide, (y + 1) * wide)
             part = convolved[i * wide : (i + 1) * wide]
-            result[line] = (hidden[line].astype(jnp.float32) + part).astype(jnp.bfloat16)
-            store = pltpu.make_async_copy(result.at[line], out.at[line], store_sem.at[y])
-            store.start()
-            stores.append(store)
-        return stores
+            out[line] = (hidden[line].astype(jnp.float32) + part).astype(jnp.bfloat16)
 
     for line in range(lines):
         place(line, activate(hidden[line * wide : (line + 1) * wide]))
-    stores = convolve(0, lines - 2)
+    convolve(0, lines - 2)
 
     @pl.when(r > 0)
     def _():
@@ -424,9 +421,12 @@
     def _():
         place(lines, jnp.zeros((wide, channels), jnp.bfloat16))
 
-    stores += convolve(lines - 2, lines)
-    for store in stores:
-        store.wait()
+    convolve(lines - 2, lines)
+
+    for which in range(2):
+        @pl.loop(1, n)
+        def _(j, which=which):
+            stat_copy(which, j).wait_send()
 
 
 def local(n, latent, attn_gain, attn_shift, w_query, w_key, w_value, w_out,
@@ -438,11 +438,14 @@
     bf16, f32 = jnp.bfloat16, jnp.float32
     square = pltpu.VMEM((channels, channels), bf16)
     dma = pltpu.SemaphoreType.DMA
+    def kept(value):
+        return pltpu.with_memory_space_constraint(value, pltpu.HBM)
+
     encoded = pl.pallas_call(
         functools.partial(kernel, n, wide),
         out_shape=jax.ShapeDtypeStruct((rows, channels), bf16),
         in_specs=[anywhere] * 11,
-        out_specs=anywhere,
+        out_specs=pl.BlockSpec(memory_space=pltpu.VMEM),
         scratch_shapes=[
             pltpu.VMEM((n // 2, chunks, 2, CHUNK, channels), bf16),
             square, square, square, square, square,
@@ -467,18 +470,16 @@
             dma((2, n)),
             dma((2,)),
             dma((2,)),
-            pltpu.VMEM((rows, channels), bf16),
-            dma((height,)),
             pltpu.VMEM((8, channels), f32),
             dma((5,)),
             pltpu.SemaphoreType.REGULAR((n // 4,)),
         ],
         compiler_params=pltpu.CompilerParams(
-            collective_id=0, has_side_effects=True, vmem_limit_bytes=56 * 1024 * 1024
+            collective_id=0, has_side_effects=True, vmem_limit_bytes=48 * 1024 * 1024
         ),
     )(
-        latent.reshape(chunks, CHUNK, channels), w_query, w_key, w_value, w_out, w_conv,
-        *(v.reshape(1, channels) for v in (attn_gain, attn_shift, conv_gain, conv_shift, conv_bias)),
+        *map(kept, (latent.reshape(chunks, CHUNK, channels), w_query, w_key, w_value, w_out, w_conv)),
+        *(kept(v.reshape(1, channels)) for v in (attn_gain, attn_shift, conv_gain, conv_shift, conv_bias)),
     )
     return encoded.reshape(height, wide, channels)
 

time: 65.8 us -> 62.8 us (0.954)
  Pallas kernels: 63.8 us -> 62 us
  local copies, waits for them, and re-layouts: 1.87 us -> 0.8 us
    pallas_call x1, Pallas kernels: 63.8 us -> 62 us  [local(): pl.pallas_call(functools.partial(kernel, n, wide), out_shape=jax.ShapeDty...]
    unnamed x1, local copies, waits for them, and re-layouts: 1.87 us -> 0.8 us
where the time goes in v5:
time: 62.8 us
  Pallas kernels  62 us (99%)
  local copies, waits for them, and re-layouts  0.8 us (1%)
    pallas_call x1, Pallas kernels, local(): pl.pallas_call(functools.partial(kernel, n, wide), out_shape=jax.ShapeDty...  62 us

profile of v5, /device:TPU:1, one launch (start us, length us, event | category | flops | bytes accessed | tf_op | source)
XLA Modules:
  0.0 62.8 jit_solution(1372979161382955906)
XLA Ops:
  0.0 62.0 %shard_map.109 = bf16[512,512]{1,0:T(8,128)(2,1)S(1)} custom-call(bf16[4,128,512]{2,1,0:T(8,128)(2,1)} %latent.1, bf16[512,512]{1,0:T(8,128)(2,1)} %w_query.1, bf16[512,512]{1,0:T(8,128)(2,1)} %w_key.1, bf16[512,512]{1,0:T(8,128)(2,1)} %w_value.1, bf16[512,512]{1,0:T(8,128)(2,1)} %w_out.1, bf16[3,3,512,512]{3,2,1,0:T(8,128)(2,1)} %w_conv.1, ...), custom_call_target="tpu_custom_call" | custom-call | tf_op jit(solution)/shard_map/pallas_call | solution.py:444
  62.0 0.8 %copy.13 = bf16[4,128,512]{2,1,0:T(8,128)(2,1)} copy(bf16[4,128,512]{2,1,0:T(8,128)(2,1)S(1)} %bitcast.6) | data formatting | bytes 1048576

commit v6 on v5

--- a/solution.py
+++ b/solution.py
@@ -37,7 +37,7 @@
     latent, w_query, w_key, w_value, w_out, w_conv,
     attn_gain_in, attn_shift_in, conv_gain_in, conv_shift_in, conv_bias_in,
     out,
-    kv, wq, wk, wv, wo, wvo, wc, ones, fold, spread, moments, queries, bias, maxima, total, acc, hidden, halo, stacked,
+    kv, mats, wvo, wc, ones, fold, spread, moments, queries, bias, maxima, total, acc, hidden, halo, stacked,
     load_sem, weight_sem, send_sem, recv_sem, stat_send, stat_recv, halo_send, halo_recv,
     vectors, vector_sem, entered,
 ):
@@ -45,6 +45,7 @@
     rows = chunks * chunk
     far = deep // 2
     half_chunks = chunks // 2
+    own_steps = half_chunks
     early = 3
     primed = 3
     lead = 3
@@ -67,85 +68,70 @@
     ]
     for load in loads:
         load.start()
-    weights = [
-        pltpu.make_async_copy(source, target, weight_sem.at[i])
-        for i, (source, target) in enumerate([(w_query, wq), (w_key, wk), (w_value, wv), (w_out, wo)])
-    ]
-    weights += [
-        pltpu.make_async_copy(
-            w_conv.at[dy, dx],
-            wc.at[dx, pl.ds(dy * channels, channels)],
-            weight_sem.at[4 + dy * 3 + dx],
-        )
-        for dy in range(3)
-        for dx in range(3)
-    ]
-    for weight in weights:
-        weight.start()
-
-    small = [
-        pltpu.make_async_copy(source, vectors.at[pl.ds(i, 1)], vector_sem.at[i])
-        for i, source in enumerate(
-            [attn_gain_in, attn_shift_in, conv_gain_in, conv_shift_in, conv_bias_in]
-        )
-    ]
-    for copy in small:
-        copy.start()
-
-    def piece(way, zb, k):
-        target = (upward, downward, partner)[way]
+    def filled(view, sem):
+        pltpu.make_async_copy(view, view, sem).wait()
+
+    for i, source in enumerate((w_query, w_key, w_value, w_out)):
+        pltpu.make_async_copy(source, mats.at[i], weight_sem.at[i // 2]).start()
+    for dy in range(3):
+        for dx in range(3):
+            pltpu.make_async_copy(
+                w_conv.at[dy, dx], wc.at[dx, pl.ds(dy * channels, channels)], weight_sem.at[2]
+            ).start()
+    for i, source in enumerate(
+        (attn_gain_in, attn_shift_in, conv_gain_in, conv_shift_in, conv_bias_in)
+    ):
+        pltpu.make_async_copy(source, vectors.at[i], vector_sem).start()
+
+    def piece(way, zb, k, mark):
         return pltpu.make_async_remote_copy(
             src_ref=kv.at[zb, k, c],
             dst_ref=kv.at[zb, k, c],
-            send_sem=send_sem.at[way, zb, k],
-            recv_sem=recv_sem.at[c, zb, k],
-            device_id=(img, target),
+            send_sem=send_sem.at[way],
+            recv_sem=recv_sem.at[way // 2, mark],
+            device_id=(img, (upward, downward, partner)[way]),
             device_id_type=MESH,
         )
 
-    def arrival(core, zb, k):
+    def whole(view, send, recv):
         return pltpu.make_async_remote_copy(
-            src_ref=kv.at[zb, k, core],
-            dst_ref=kv.at[zb, k, core],
-            send_sem=send_sem.at[0, 0, 0],
-            recv_sem=recv_sem.at[core, zb, k],
+            src_ref=view,
+            dst_ref=view,
+            send_sem=send,
+            recv_sem=recv,
             device_id=(img, partner),
             device_id_type=MESH,
         )
+
+    def arrived(relayed, s):
+        pair = kv.at[0, 0]
+        whole(pair, send_sem.at[0], recv_sem.at[relayed, s]).wait_recv()
 
     def stat_copy(which, j):
         return pltpu.make_async_remote_copy(
             src_ref=moments.at[which, r],
             dst_ref=moments.at[which, r],
-            send_sem=stat_send.at[which, j],
-            recv_sem=stat_recv.at[which, r],
+            send_sem=stat_send.at[which],
+            recv_sem=stat_recv.at[which],
             device_id=(img, lax.rem(r + j, n)),
             device_id_type=MESH,
         )
 
-    def stat_arrival(which, b):
-        return pltpu.make_async_remote_copy(
-            src_ref=moments.at[which, b],
-            dst_ref=moments.at[which, b],
-            send_sem=stat_send.at[which, 0],
-            recv_sem=stat_recv.at[which, b],
-            device_id=(img, partner),
-            device_id_type=MESH,
-        )
+    def stat_all(which):
+        view = moments.at[which, pl.ds(0, n - 1)]
+        return whole(view, stat_send.at[which], stat_recv.at[which])
 
     def own():
         return kv[z, :, c]
 
     def send_own(k):
-        piece(0, z, k).start()
-        piece(1, z, k).start()
-        piece(2, z, k).start()
+        piece(0, z, k, own_steps + k).start()
+        piece(1, z, k, own_steps + k).start()
+        piece(2, z, k, k // 2).start()
 
     def split(way, d, k):
         part = (k < half_chunks) if way == 0 else (k >= half_chunks)
         return jnp.logical_or(d < far, jnp.logical_and(d == far, part))
-
-    own_steps = half_chunks
 
     def spot(way, s):
         e = s - own_steps
@@ -156,15 +142,16 @@
         return d, zb, step
 
     def relay(s):
+        arrived(0, s)
         for way in (0, 1):
             d, zb, k = spot(way, s)
-            arrival(c, zb, k).wait_recv()
+            mark = s + chunks - jnp.where(d + 1 == far, way * half_chunks, 0)
 
             @pl.when(split(way, d + 1, k))
-            def _(way=way, zb=zb, k=k):
-                piece(way, zb, k).start()
-
-            piece(2, zb, k).start()
+            def _(way=way, zb=zb, k=k, mark=mark):
+                piece(way, zb, k, mark).start()
+
+            piece(2, zb, k, s).start()
 
     def share_moments(which, field):
         mean = jnp.sum(field, axis=0, keepdims=True) * (1.0 / rows)
@@ -181,10 +168,7 @@
             stat_copy(which, j).start()
 
     def gather_moments(which):
-        @pl.loop(1, n)
-        def _(j):
-            stat_arrival(which, lax.rem(r + j, n)).wait_recv()
-
+        stat_all(which).wait_recv()
         every = moments[which]
         means = every[:, 0, :]
         squares = every[:, 1, :]
@@ -230,27 +214,24 @@
     for s in range(own_steps, own_steps + primed):
         relay(s)
 
-    for weight in weights[:2]:
-        weight.wait()
-    for copy in small:
-        copy.wait()
-    attn_gain, attn_shift, conv_gain, conv_shift = (vectors[i : i + 1] for i in range(4))
-    conv_bias = vectors.at[4:5]
+    filled(mats.at[pl.ds(0, 2)], weight_sem.at[0])
+    filled(vectors, vector_sem)
+    attn_gain, attn_shift, conv_gain, conv_shift = (vectors[i] for i in range(4))
+    conv_bias = vectors[4]
     centre, scale = gather_moments(0)
     gain = scale * attn_gain
     positions = own().reshape(rows, channels).astype(jnp.float32)
     normed = ((positions - centre) * gain + attn_shift).astype(jnp.bfloat16)
-    query = jnp.dot(normed, wq[...], preferred_element_type=jnp.float32).astype(jnp.bfloat16)
-    folded = lax.dot_general(query, wk[...], NT, preferred_element_type=jnp.float32) * (
+    query = jnp.dot(normed, mats[0], preferred_element_type=jnp.float32).astype(jnp.bfloat16)
+    folded = lax.dot_general(query, mats[1], NT, preferred_element_type=jnp.float32) * (
         LOG2E / math.sqrt(channels)
     )
     queries[...] = (folded * gain).astype(jnp.bfloat16)
     constant = jnp.sum(folded * (attn_shift - centre * gain), axis=1, keepdims=True)
     bias[...] = jnp.broadcast_to(constant, bias.shape)
 
-    for weight in weights[2:4]:
-        weight.wait()
-    wvo[...] = jnp.dot(wv[...], wo[...], preferred_element_type=jnp.float32).astype(jnp.bfloat16)
+    filled(mats.at[pl.ds(2, 2)], weight_sem.at[1])
+    wvo[...] = jnp.dot(mats[2], mats[3], preferred_element_type=jnp.float32).astype(jnp.bfloat16)
 
     lanes = 128
     halves = [slice(i, i + rows // 2) for i in range(0, rows, rows // 2)]
@@ -298,18 +279,17 @@
         def _():
             relay(s)
 
+        arrived(1, s)
         blocks = []
         for way in (0, 1):
             d, zb, k = spot(way, s)
-            arrival(1 - c, zb, k).wait_recv()
             blocks.append(kv[zb, k].reshape(2 * chunk, channels))
         attend(blocks)
 
     final = [spot(way, steps - 1) for way in (0, 1)]
     relay(steps - 1)
     attend([jnp.concatenate([kv[zb, k, c] for d, zb, k in final], axis=0)])
-    for d, zb, k in final:
-        arrival(1 - c, zb, k).wait_recv()
+    arrived(1, steps - 1)
     attend([jnp.concatenate([kv[zb, k, 1 - c] for d, zb, k in final], axis=0)])
 
     denominator = jnp.sum(total[...], axis=1, keepdims=True)
@@ -346,23 +326,12 @@
     def _():
         down.start()
 
-    @pl.loop(0, deep * chunks)
-    def _(t):
-        zb = t // chunks
-        k = t % chunks
-
-        @pl.when(split(0, lax.rem(z + deep - zb, deep) + 1, k))
-        def _():
-            piece(0, zb, k).wait_send()
-
-        @pl.when(split(1, lax.rem(zb + deep - z, deep) + 1, k))
-        def _():
-            piece(1, zb, k).wait_send()
-
-        piece(2, zb, k).wait_send()
-
-    for weight in weights[4:]:
-        weight.wait()
+    along = kv.at[pl.ds(0, (steps - own_steps) // 2), pl.ds(0, 1)]
+    across = kv.at[pl.ds(0, deep // 2)]
+    for way, view in enumerate((along, along, across)):
+        whole(view, send_sem.at[way], recv_sem.at[0, 0]).wait_send()
+
+    filled(wc, weight_sem.at[2])
     centre, scale = gather_moments(1)
     gain = scale * conv_gain
 
@@ -387,7 +356,7 @@
         def taps(dx):
             return jnp.dot(window, wc[dx], preferred_element_type=jnp.float32)
 
-        convolved = taps(1) + conv_bias[...]
+        convolved = taps(1) + conv_bias
         convolved = convolved + jnp.where(column > 0, pltpu.roll(taps(0), 1, 0), 0.0)
         convolved = convolved + jnp.where(
             column < wide - 1, pltpu.roll(taps(2), count - 1, 0), 0.0
@@ -424,9 +393,7 @@
     convolve(lines - 2, lines)
 
     for which in range(2):
-        @pl.loop(1, n)
-        def _(j, which=which):
-            stat_copy(which, j).wait_send()
+        stat_all(which).wait_send()
 
 
 def local(n, latent, attn_gain, attn_shift, w_query, w_key, w_value, w_out,
@@ -448,7 +415,8 @@
         out_specs=pl.BlockSpec(memory_space=pltpu.VMEM),
         scratch_shapes=[
             pltpu.VMEM((n // 2, chunks, 2, CHUNK, channels), bf16),
-            square, square, square, square, square,
+            pltpu.VMEM((4, channels, channels), bf16),
+            square,
             pltpu.VMEM((3, 3 * channels, channels), bf16),
             square,
             pltpu.VMEM((channels, 128), bf16),
@@ -463,15 +431,15 @@
             pltpu.VMEM((2, wide, channels), bf16),
             pltpu.VMEM((rows, 3 * channels), bf16),
             dma((chunks,)),
-            dma((13,)),
-            dma((3, n // 2, chunks)),
-            dma((2, n // 2, chunks)),
-            dma((2, n)),
+            dma((3,)),
+            dma((3,)),
             dma((2, n)),
             dma((2,)),
             dma((2,)),
-            pltpu.VMEM((8, channels), f32),
-            dma((5,)),
+            dma((2,)),
+            dma((2,)),
+            pltpu.VMEM((5, 1, channels), f32),
+            dma,
             pltpu.SemaphoreType.REGULAR((n // 4,)),
         ],
         compiler_params=pltpu.CompilerParams(

time: 62.8 us -> 60.9 us (0.970)
  Pallas kernels: 62 us -> 60 us
    pallas_call x1, Pallas kernels: 62 us -> 60 us  [local(): pl.pallas_call(functools.partial(kernel, n, wide), out_shape=jax.ShapeDty...]
where the time goes in v6:
time: 60.9 us; the launch traced here: 60.8 us
  Pallas kernels  60 us (99%)
  local copies, waits for them, and re-layouts  0.8 us (1%)
    pallas_call x1, Pallas kernels, local(): pl.pallas_call(functools.partial(kernel, n, wide), out_shape=jax.ShapeDty...  60 us

profile of v6, /device:TPU:1, one launch (start us, length us, event | category | flops | bytes accessed | tf_op | source)
XLA Modules:
  0.0 60.8 jit_solution(15456907316073383992)
XLA Ops:
  0.0 60.0 %shard_map.109 = bf16[512,512]{1,0:T(8,128)(2,1)S(1)} custom-call(bf16[4,128,512]{2,1,0:T(8,128)(2,1)} %latent.1, bf16[512,512]{1,0:T(8,128)(2,1)} %w_query.1, bf16[512,512]{1,0:T(8,128)(2,1)} %w_key.1, bf16[512,512]{1,0:T(8,128)(2,1)} %w_value.1, bf16[512,512]{1,0:T(8,128)(2,1)} %w_out.1, bf16[3,3,512,512]{3,2,1,0:T(8,128)(2,1)} %w_conv.1, ...), custom_call_target="tpu_custom_call" | custom-call | tf_op jit(solution)/shard_map/pallas_call | solution.py:411
  60.0 0.8 %copy.13 = bf16[4,128,512]{2,1,0:T(8,128)(2,1)} copy(bf16[4,128,512]{2,1,0:T(8,128)(2,1)S(1)} %bitcast.6) | data formatting | bytes 1048576

commit v7 on v6

--- a/solution.py
+++ b/solution.py
@@ -39,7 +39,7 @@
     out,
     kv, mats, wvo, wc, ones, fold, spread, moments, queries, bias, maxima, total, acc, hidden, halo, stacked,
     load_sem, weight_sem, send_sem, recv_sem, stat_send, stat_recv, halo_send, halo_recv,
-    vectors, vector_sem, entered,
+    vectors, vector_sem, entered, mixed, edge,
 ):
     deep, chunks, _, chunk, channels = kv.shape
     rows = chunks * chunk
@@ -76,7 +76,7 @@
     for dy in range(3):
         for dx in range(3):
             pltpu.make_async_copy(
-                w_conv.at[dy, dx], wc.at[dx, pl.ds(dy * channels, channels)], weight_sem.at[2]
+                w_conv.at[dy, dx], wc.at[dy, pl.ds(dx * channels, channels)], weight_sem.at[2]
             ).start()
     for i, source in enumerate(
         (attn_gain_in, attn_shift_in, conv_gain_in, conv_shift_in, conv_bias_in)
@@ -163,8 +163,7 @@
         moments[which, r, 0:1, :] = sums * (1.0 / size)
         moments[which, r, 1:2, :] = squares
 
-        @pl.loop(1, n)
-        def _(j):
+        for j in sorted(range(1, n), key=lambda j: abs(j - n // 2)):
             stat_copy(which, j).start()
 
     def gather_moments(which):
@@ -232,6 +231,16 @@
 
     filled(mats.at[pl.ds(2, 2)], weight_sem.at[1])
     wvo[...] = jnp.dot(mats[2], mats[3], preferred_element_type=jnp.float32).astype(jnp.bfloat16)
+
+    filled(wc, weight_sem.at[2])
+
+    @pl.loop(0, 3)
+    def _(dx):
+        part = pl.ds(pl.multiple_of(dx * channels, channels), channels)
+        outer = wc[0, part].astype(jnp.float32) + wc[2, part].astype(jnp.float32)
+        inner = wc[1, part].astype(jnp.float32)
+        mixed[0, part] = (0.5 * (outer + inner)).astype(jnp.bfloat16)
+        mixed[1, part] = (0.5 * (outer - inner)).astype(jnp.bfloat16)
 
     lanes = 128
     halves = [slice(i, i + rows // 2) for i in range(0, rows, rows // 2)]
@@ -331,66 +340,69 @@
     for way, view in enumerate((along, along, across)):
         whole(view, send_sem.at[way], recv_sem.at[0, 0]).wait_send()
 
-    filled(wc, weight_sem.at[2])
     centre, scale = gather_moments(1)
     gain = scale * conv_gain
 
     def activate(values):
         v = (values.astype(jnp.float32) - centre) * gain + conv_shift
-        return (v / (1.0 + jnp.exp(-v))).astype(jnp.bfloat16)
-
-    order = [*range(1, lines - 1), 0, lines - 1]
-
-    def place(line, values):
-        for dy in range(3):
-            y = line + 1 - dy
-            if 0 <= y < lines:
-                slot = order.index(y) * wide
-                stacked[slot : slot + wide, dy * channels : (dy + 1) * channels] = values
-
-    def convolve(first, last):
-        count = (last - first) * wide
-        window = stacked[first * wide : last * wide]
-        column = lax.broadcasted_iota(jnp.int32, (count, channels), 0) % wide
-
-        def taps(dx):
-            return jnp.dot(window, wc[dx], preferred_element_type=jnp.float32)
-
-        convolved = taps(1) + conv_bias
-        convolved = convolved + jnp.where(column > 0, pltpu.roll(taps(0), 1, 0), 0.0)
-        convolved = convolved + jnp.where(
-            column < wide - 1, pltpu.roll(taps(2), count - 1, 0), 0.0
-        )
-        for i, y in enumerate(order[first:last]):
-            line = slice(y * wide, (y + 1) * wide)
-            part = convolved[i * wide : (i + 1) * wide]
-            out[line] = (hidden[line].astype(jnp.float32) + part).astype(jnp.bfloat16)
-
-    for line in range(lines):
-        place(line, activate(hidden[line * wide : (line + 1) * wide]))
-    convolve(0, lines - 2)
+        return (v / (1.0 + jnp.exp(-v))).astype(jnp.bfloat16).astype(jnp.float32)
+
+    column = lax.broadcasted_iota(jnp.int32, (wide, channels), 0)
+
+    def place(term, pair, values):
+        at = slice(pair * wide, (pair + 1) * wide)
+        before = jnp.where(column > 0, pltpu.roll(values, 1, 0), 0.0)
+        after = jnp.where(column < wide - 1, pltpu.roll(values, wide - 1, 0), 0.0)
+        for dx, part in enumerate((before, values, after)):
+            stacked[term, at, dx * channels : (dx + 1) * channels] = part.astype(jnp.bfloat16)
+
+    def product(term, matrix):
+        return jnp.dot(stacked[term], matrix, preferred_element_type=jnp.float32)
+
+    first, second, third, fourth = (
+        activate(hidden[y * wide : (y + 1) * wide]) for y in range(lines)
+    )
+    edge[0] = second
+    edge[1] = third
+    for pair, (upper, lower) in enumerate(((first, second), (third, fourth))):
+        place(1, pair, upper + lower)
+        place(2, pair, lower - upper)
+    place(0, 1, second - fourth)
+    place(3, 0, first - third)
+    sums, gaps = product(1, mixed[0]), product(2, mixed[1])
+    acc[: rows // 2] = sums + gaps
+    acc[rows // 2 :] = sums - gaps
 
     @pl.when(r > 0)
     def _():
         up.wait_send()
         down.wait_recv()
-        place(-1, activate(halo[0]))
+        edge[2] = activate(halo[0])
 
     @pl.when(r == 0)
     def _():
-        place(-1, jnp.zeros((wide, channels), jnp.bfloat16))
+        edge[2] = jnp.zeros((wide, channels), jnp.float32)
 
     @pl.when(r < n - 1)
     def _():
         down.wait_send()
         up.wait_recv()
-        place(lines, activate(halo[1]))
+        edge[3] = activate(halo[1])
 
     @pl.when(r == n - 1)
     def _():
-        place(lines, jnp.zeros((wide, channels), jnp.bfloat16))
-
-    convolve(lines - 2, lines)
+        edge[3] = jnp.zeros((wide, channels), jnp.float32)
+
+    place(0, 0, edge[2] - edge[0])
+    place(3, 1, edge[1] - edge[3])
+    evens = acc[: rows // 2] + product(0, wc[0])
+    odds = acc[rows // 2 :] - product(3, wc[2])
+    for parity, values in enumerate((evens, odds)):
+        for pair in range(2):
+            y = 2 * pair + parity
+            line = slice(y * wide, (y + 1) * wide)
+            part = values[pair * wide : (pair + 1) * wide] + conv_bias
+            out[line] = (hidden[line].astype(jnp.float32) + part).astype(jnp.bfloat16)
 
     for which in range(2):
         stat_all(which).wait_send()
@@ -429,7 +441,7 @@
             pltpu.VMEM((rows, channels), f32),
             pltpu.VMEM((rows, channels), bf16),
             pltpu.VMEM((2, wide, channels), bf16),
-            pltpu.VMEM((rows, 3 * channels), bf16),
+            pltpu.VMEM((4, rows // 2, 3 * channels), bf16),
             dma((chunks,)),
             dma((3,)),
             dma((3,)),
@@ -441,6 +453,8 @@
             pltpu.VMEM((5, 1, channels), f32),
             dma,
             pltpu.SemaphoreType.REGULAR((n // 4,)),
+            pltpu.VMEM((2, 3 * channels, channels), bf16),
+            pltpu.VMEM((4, wide, channels), f32),
         ],
         compiler_params=pltpu.CompilerParams(
             collective_id=0, has_side_effects=True, vmem_limit_bytes=48 * 1024 * 1024

time: 60.9 us -> 60.3 us (level)
  no operation moved by 1% of the time
where the time goes in v7:
time: 60.3 us
  Pallas kernels  59.5 us (99%)
  local copies, waits for them, and re-layouts  0.8 us (1%)
    pallas_call x1, Pallas kernels, local(): pl.pallas_call(functools.partial(kernel, n, wide), out_shape=jax.ShapeDty...  59.5 us

profile of v7, /device:TPU:1, one launch (start us, length us, event | category | flops | bytes accessed | tf_op | source)
XLA Modules:
  0.0 60.3 jit_solution(10994596808371838665)
XLA Ops:
  0.0 59.5 %shard_map.109 = bf16[512,512]{1,0:T(8,128)(2,1)S(1)} custom-call(bf16[4,128,512]{2,1,0:T(8,128)(2,1)} %latent.1, bf16[512,512]{1,0:T(8,128)(2,1)} %w_query.1, bf16[512,512]{1,0:T(8,128)(2,1)} %w_key.1, bf16[512,512]{1,0:T(8,128)(2,1)} %w_value.1, bf16[512,512]{1,0:T(8,128)(2,1)} %w_out.1, bf16[3,3,512,512]{3,2,1,0:T(8,128)(2,1)} %w_conv.1, ...), custom_call_target="tpu_custom_call" | custom-call | tf_op jit(solution)/shard_map/pallas_call | solution.py:423
  59.5 0.8 %copy.13 = bf16[4,128,512]{2,1,0:T(8,128)(2,1)} copy(bf16[4,128,512]{2,1,0:T(8,128)(2,1)S(1)} %bitcast.6) | data formatting | bytes 1048576

commit v8 on v7

--- a/solution.py
+++ b/solution.py
@@ -315,7 +315,7 @@
         dst_ref=halo.at[1],
         send_sem=halo_send.at[1],
         recv_sem=halo_recv.at[1],
-        device_id=(img, r - 1),
+        device_id=(img, lax.rem(r + n - 1, n)),
         device_id_type=MESH,
     )
     down = pltpu.make_async_remote_copy(
@@ -323,7 +323,7 @@
         dst_ref=halo.at[0],
         send_sem=halo_send.at[0],
         recv_sem=halo_recv.at[0],
-        device_id=(img, r + 1),
+        device_id=(img, lax.rem(r + 1, n)),
         device_id_type=MESH,
     )
 

time: 60.3 us -> 60.3 us (level)
  no operation moved by 1% of the time
where the time goes in v8:
time: 60.3 us
  Pallas kernels  59.5 us (99%)
  local copies, waits for them, and re-layouts  0.8 us (1%)
    pallas_call x1, Pallas kernels, local(): pl.pallas_call(functools.partial(kernel, n, wide), out_shape=jax.ShapeDty...  59.5 us

profile of v8, /device:TPU:1, one launch (start us, length us, event | category | flops | bytes accessed | tf_op | source)
XLA Modules:
  0.0 60.3 jit_solution(8931143666550205023)
XLA Ops:
  0.0 59.5 %shard_map.109 = bf16[512,512]{1,0:T(8,128)(2,1)S(1)} custom-call(bf16[4,128,512]{2,1,0:T(8,128)(2,1)} %latent.1, bf16[512,512]{1,0:T(8,128)(2,1)} %w_query.1, bf16[512,512]{1,0:T(8,128)(2,1)} %w_key.1, bf16[512,512]{1,0:T(8,128)(2,1)} %w_value.1, bf16[512,512]{1,0:T(8,128)(2,1)} %w_out.1, bf16[3,3,512,512]{3,2,1,0:T(8,128)(2,1)} %w_conv.1, ...), custom_call_target="tpu_custom_call" | custom-call | tf_op jit(solution)/shard_map/pallas_call | solution.py:423
  59.5 0.8 %copy.13 = bf16[4,128,512]{2,1,0:T(8,128)(2,1)} copy(bf16[4,128,512]{2,1,0:T(8,128)(2,1)S(1)} %bitcast.6) | data formatting | bytes 1048576

commit v9 on v8

--- a/solution.py
+++ b/solution.py
@@ -64,7 +64,7 @@
         pl.semaphore_signal(barrier, inc=1, device_id=(img, target), device_id_type=MESH)
 
     loads = [
-        pltpu.make_async_copy(latent.at[k], kv.at[z, k, c], load_sem.at[k]) for k in range(chunks)
+        pltpu.make_async_copy(latent.at[k], kv.at[z, k, c], load_sem) for k in range(chunks)
     ]
     for load in loads:
         load.start()
@@ -178,8 +178,8 @@
         return exact_dot([centre, scale], spread[...])
 
     pl.semaphore_wait(barrier, 3)
+    filled(kv.at[z, :, c], load_sem)
     for k in range(chunks):
-        loads[k].wait()
         if k < early:
             send_own(k)
     def groups(shape, left, right):
@@ -442,7 +442,7 @@
             pltpu.VMEM((rows, channels), bf16),
             pltpu.VMEM((2, wide, channels), bf16),
             pltpu.VMEM((4, rows // 2, 3 * channels), bf16),
-            dma((chunks,)),
+            dma,
             dma((3,)),
             dma((3,)),
             dma((2, n)),

time: 60.3 us -> 60.8 us (level)
  no operation moved by 1% of the time
where the time goes in v9:
time: 60.8 us; the launch traced here: 60.7 us
  Pallas kernels  59.9 us (99%)
  local copies, waits for them, and re-layouts  0.8 us (1%)
    pallas_call x1, Pallas kernels, local(): pl.pallas_call(functools.partial(kernel, n, wide), out_shape=jax.ShapeDty...  59.9 us

profile of v9, /device:TPU:1, one launch (start us, length us, event | category | flops | bytes accessed | tf_op | source)
XLA Modules:
  0.0 60.7 jit_solution(10658649464202551555)
XLA Ops:
  0.0 59.9 %shard_map.109 = bf16[512,512]{1,0:T(8,128)(2,1)S(1)} custom-call(bf16[4,128,512]{2,1,0:T(8,128)(2,1)} %latent.1, bf16[512,512]{1,0:T(8,128)(2,1)} %w_query.1, bf16[512,512]{1,0:T(8,128)(2,1)} %w_key.1, bf16[512,512]{1,0:T(8,128)(2,1)} %w_value.1, bf16[512,512]{1,0:T(8,128)(2,1)} %w_out.1, bf16[3,3,512,512]{3,2,1,0:T(8,128)(2,1)} %w_conv.1, ...), custom_call_target="tpu_custom_call" | custom-call | tf_op jit(solution)/shard_map/pallas_call | solution.py:423
  59.9 0.8 %copy.13 = bf16[4,128,512]{2,1,0:T(8,128)(2,1)} copy(bf16[4,128,512]{2,1,0:T(8,128)(2,1)S(1)} %bitcast.6) | data formatting | bytes 1048576
